TPU v7x, 512 devices: a 4x2x32 block of a 4x8x32 slice. The times are simulated.
512 devices in a mesh: group: 2 (over y), ctx: 32 (over z), head: 4 (over x), dec: 2 (over core).
Axes of the slice: x: 4, y: 2, z: 32, core: 2. Of those that a mesh axis runs over, the one named last changes fastest.
The devices are a block of a 4x8x32 slice.
Arguments:
- queries: bfloat16 [8192, 12288], P(('group', 'ctx'), ('head', 'dec')), parts along dimension 0, may hold values from -1100 to 1100
- latent_rows: bfloat16 [8192, 576], P(('group', 'ctx')), parts along dimension 0, may hold values from -8 to 8
- segments: int32 [8192], P('group'), parts along dimension 0, may hold values from 0 to 3, never falling along the last dimension, each value on 1 to 2048 neighbouring positions
- owners: int32 [8192, 1], P(('group', 'ctx')), parts along dimension 0, may hold values from 0 to 63; in each aligned block of 128 rows (0 to 127, 128 to 255, ...) at most 4 rows name the same one
- absorb_key: bfloat16 [64, 128, 512], P(('head', 'dec')), may hold values from -0.5 to 0.5
- absorb_value: bfloat16 [64, 512, 128], P(('head', 'dec')), may hold values from -0.25 to 0.25
Outputs:
- attended: bfloat16 [8192, 8192], P(('group', 'ctx'), ('head', 'dec')), parts along dimension 0
- kv_cache: bfloat16 [128, 32, 4, 576], P(('group', 'ctx', 'dec')), parts along dimension 0
There are 2 independent parts, one for each index of `group`. A program takes and returns all parts, laid end to end along the dimension named above; an argument that names none is the same for every part. Nothing has to cross between parts.
Inputs may be any that keep to these rules, and one draw needn't show every extreme that they name: `segments`: prompt numbers never fall along the tokens; each prompt has 1 to 2048 tokens and one has exactly 2048. `owners`: among the 128 tokens of one index of ctx no owner is named more than 4 times; some owner is named exactly 4 times in some of them; every owner is named somewhere.
All inputs are finite; a program needn't handle non-finite values.
Results may differ from a plain program's by a relative error of at most 0.0085.
Values may be sent and summed in bfloat16 or wider, within the bound.
No kernel may reach another device: no remote copies, remote signals or barrier semaphores. Data moves between devices by JAX's collectives and lax.ppermute only.
A program may use at most 128 MiB of HBM per device.

v0:
```python
import jax
import jax.numpy as jnp
from jax import lax
from jax.sharding import PartitionSpec as P

NOPE = 128
ROPE = 64
LATENT = 512
VDIM = 128


def rotate_pairs(rope_part, positions):
    half_rope = ROPE // 2
    frequency = 10000.0 ** (-jnp.arange(half_rope, dtype=jnp.float32) * 2.0 / ROPE)
    angles = positions.astype(jnp.float32)[:, None] * frequency[None, :]
    cosine = jnp.cos(angles)[:, None, :]
    sine_part = jnp.sin(angles)[:, None, :]
    first_part = rope_part[..., :half_rope]
    second = rope_part[..., half_rope:]
    return jnp.concatenate(
        [first_part * cosine - second * sine_part, first_part * sine_part + second * cosine],
        axis=-1,
    )


def ship_rows(latent_rows, owners):
    row_count = latent_rows.shape[0]
    ctx_count = lax.axis_size("ctx")
    dec_count = lax.axis_size("dec")
    core_index = lax.axis_index("dec")
    slots = max(2, 2 * row_count // (ctx_count * dec_count))
    owner_ids = owners[:, 0]
    row_order = jnp.arange(row_count, dtype=jnp.int32)
    earlier = row_order[None, :] < row_order[:, None]
    slot_rank = jnp.sum((owner_ids[:, None] == owner_ids[None, :]) & earlier, axis=1)
    target = owner_ids // dec_count * slots + slot_rank
    kept_rows = owner_ids % dec_count == core_index
    picker = (
        (jnp.arange(ctx_count * slots, dtype=jnp.int32)[:, None] == target[None, :])
        & kept_rows[None, :]
    ).astype(jnp.bfloat16)
    outgoing = jnp.dot(picker, latent_rows, preferred_element_type=jnp.float32).astype(jnp.bfloat16)
    outgoing = outgoing.reshape(ctx_count, slots, LATENT + ROPE)
    arrived = lax.all_to_all(outgoing, "ctx", split_axis=0, concat_axis=0, tiled=True)
    return arrived[None]


def on_device(queries, latent_rows, segments, owners, absorb_key, absorb_value):
    row_count = queries.shape[0]
    local_heads = absorb_key.shape[0]
    width = LATENT + ROPE
    ctx_index = lax.axis_index("ctx")
    scale = (NOPE + ROPE) ** (-0.5)
    shaped = queries.reshape(row_count, local_heads, NOPE + ROPE)
    offsets = jnp.arange(row_count, dtype=jnp.int32)
    query_pos = ctx_index * row_count + offsets
    query_seg = jnp.take(segments, query_pos)
    rotated = rotate_pairs(shaped[..., NOPE:].astype(jnp.float32), query_pos).astype(jnp.bfloat16)
    absorbed = jnp.einsum(
        "thn,hnc->thc", shaped[..., :NOPE], absorb_key, preferred_element_type=jnp.float32
    ).astype(jnp.bfloat16)
    full_query = jnp.concatenate([absorbed, rotated], axis=-1).reshape(
        row_count * local_heads, width
    )
    last_query = jnp.max(query_pos)
    lowest_seg = jnp.min(query_seg)
    highest_seg = jnp.max(query_seg)
    start_state = (
        jnp.full((row_count, local_heads), -1e30, jnp.float32),
        jnp.zeros((row_count, local_heads), jnp.float32),
        jnp.zeros((row_count, local_heads, LATENT), jnp.float32),
    )
    key_piece = lax.all_gather(latent_rows, "ctx", axis=0, tiled=True)
    count = key_piece.shape[0]
    key_pos = jnp.arange(count, dtype=jnp.int32)
    is_live = (
        (jnp.int32(0) <= last_query)
        & (segments[count - 1] >= lowest_seg)
        & (segments[0] <= highest_seg)
    )

    def update(carried):
        running_max, running_sum, running_out = carried
        scores = jnp.einsum("qw,kw->qk", full_query, key_piece, preferred_element_type=jnp.float32)
        scores = scores.reshape(row_count, local_heads, count) * scale
        allowed = (
            (key_pos[None, :] <= query_pos[:, None]) & (segments[None, :] == query_seg[:, None])
        )[:, None, :]
        masked = jnp.where(allowed, scores, -1e30)
        new_max = jnp.maximum(running_max, jnp.max(masked, axis=2))
        weights = jnp.where(allowed, jnp.exp(masked - new_max[..., None]), 0.0)
        new_sum = jnp.sum(weights, axis=2)
        mixed = jnp.dot(
            weights.astype(jnp.bfloat16).reshape(row_count * local_heads, count),
            key_piece[:, :LATENT],
            preferred_element_type=jnp.float32,
        )
        new_out = mixed.reshape(row_count, local_heads, LATENT)
        return (new_max, new_sum, new_out)

    final_state = lax.cond(is_live, update, lambda carried: carried, start_state)
    running_max, running_sum, running_out = final_state
    latent_out = (running_out / running_sum[..., None]).astype(jnp.bfloat16)
    answer = jnp.einsum(
        "thc,hcv->thv", latent_out, absorb_value, preferred_element_type=jnp.float32
    ).astype(jnp.bfloat16)
    answer = answer.reshape(row_count, local_heads * VDIM)
    kv_cache = ship_rows(latent_rows, owners)
    return (answer, kv_cache)


def solution(mesh):
    in_specs = (
        P(("group", "ctx"), ("head", "dec")),
        P(("group", "ctx"), None),
        P("group"),
        P(("group", "ctx"), None),
        P(("head", "dec"), None, None),
        P(("head", "dec"), None, None),
    )
    out_specs = (P(("group", "ctx"), ("head", "dec")), P(("group", "ctx", "dec"), None, None, None))
    return jax.shard_map(
        on_device, mesh=mesh, in_specs=in_specs, out_specs=out_specs, check_vma=False
    )
```

profile of v0, /device:TPU:44, one launch (start us, length us, event | category | flops | bytes accessed | tf_op | source)
XLA Modules:
  0.0 235.0 jit_solution(2218947732454641080)
XLA Ops:
  7.2 0.0 copy-start
  7.2 0.1 all-gather.2.cloned.1.call-start
  7.3 1.8 copy.31
  9.1 0.1 all-gather.2.cloned.1.call-update
  9.1 0.9 convert_reduce_fusion
  10.0 0.7 fusion.22
  10.7 0.7 multiply_add_fusion
  11.4 1.1 convolution_convert_fusion.2
  12.5 0.2 copy.35
  12.6 0.7 reshape.219
  13.4 45.8 %all-to-all-start = ((bf16[32,4,576]{2,1,0:T(4,128)(2,1)}), bf16[32,4,576]{2,1,0:T(4,128)(2,1)S(1)}, u32[]{:S(2)}, u32[]{:S(2)}) async-start(bf16[32,4,576]{2,1,0:T(4,128)(2,1)} %reshape.219), calls=%async_computation | async-start | bytes 327680 | tf_op jit(solution)/shard_map/all_to_all | solution.py:44
  59.2 1.6 gather_fusion
  60.8 0.7 fusion.24
  61.5 1.3 fusion.27
  62.9 0.7 fusion.26
  63.6 1.2 copy.28
  67.9 0.1 multiply_cosine_fusion
  68.2 0.5 fusion.14
  68.7 1.1 pad_maximum_fusion
  69.8 24.9 %all-to-all-done = bf16[32,4,576]{2,1,0:T(4,128)(2,1)S(1)} async-done(((bf16[32,4,576]{2,1,0:T(4,128)(2,1)}), bf16[32,4,576]{2,1,0:T(4,128)(2,1)S(1)}, u32[]{:S(2)}, u32[]{:S(2)}) %all-to-all-start) | async-done | bytes 147488 | tf_op jit(solution)/shard_map/all_to_all | solution.py:44
  94.7 93.2 %all-gather.2.cloned.1.call-done = bf16[4096,576]{1,0:T(8,128)(2,1)} async-done(((bf16[128,576]{1,0:T(8,128)(2,1)}), bf16[4096,576]{1,0:T(8,128)(2,1)}) %all-gather.2.cloned.1.call-update) | async-done | bytes 4718608 | tf_op jit(solution)/shard_map/all_gather | solution.py:73
  187.9 36.4 %conditional.1 = (f32[128,8]{1,0:T(8,128)S(1)}, f32[128,8,512]{2,1,0:T(8,128)S(1)}) conditional(s32[]{:T(128)} %convert_element_type.40, () %tuple.16, (s32[4096]{0:T(1024)S(1)}, s32[128]{0:T(128)S(1)}, s32[4096]{0:T(1024)S(1)}, s32[128]{0:T(128)S(1)}, bf16[128,8,576]{0,2,1:T(8,128)(2,1)}, /*index=5*/bf16[4096,576]{1,0:T(8,128)(2,1)}) %tuple.39), branch_computations={%region_3.4_spmd, %region_4.0_spmd} | conditional | flops 9182903296 | bytes 71238728 | solution.py:101
  187.9 0.5 compare_and_fusion
  188.4 2.4 %copy.32 = bf16[128,8,576]{2,1,0:T(8,128)(2,1)S(1)} copy(bf16[128,8,576]{0,2,1:T(8,128)(2,1)} %get-tuple-element.45) | data formatting | bytes 2359296 | tf_op jit(solution)/shard_map
  190.8 13.9 %fusion = (f32[1024]{0:T(1024)S(1)}, f32[1024,4096]{1,0:T(8,128)}) fusion(pred[128,4096]{1,0:T(8,128)(4,1)S(1)} %compare_and_fusion, bf16[4096,576]{1,0:T(8,128)(2,1)} %get-tuple-element.18, bf16[128,8,576]{2,1,0:T(8,128)(2,1)S(1)} %copy.32), kind=kOutput, calls=%fused_computation.3 | convolution fusion | flops 4844420096 | bytes 23203840 | tf_op jit(solution)/shard_map/cond/branch_1_fun/qw,kw->qk/dot_general | solution.py:84
  204.7 10.4 %fusion.4 = f32[128,8,512]{2,1,0:T(8,128)S(1)} fusion(f32[1024,4096]{1,0:T(8,128)} %get-tuple-element.53, f32[1024]{0:T(1024)S(1)} %broadcast_maximum_fusion, pred[128,4096]{1,0:T(8,128)(4,1)} %copy-done.2, bf16[4096,576]{1,0:T(8,128)(2,1)} %get-tuple-element.18), kind=kOutput, calls=%fused_computation.7 | convolution fusion | flops 4315938816 | bytes 23597056 | tf_op jit(solution)/shard_map/cond/branch_1_fun/dot_general | solution.py:93
  215.1 9.1 %fusion.2 = f32[1024]{0:T(1024)S(1)} fusion(f32[1024,4096]{1,0:T(8,128)} %get-tuple-element.53, f32[1024]{0:T(1024)S(1)} %broadcast_maximum_fusion, pred[128,4096]{1,0:T(8,128)(4,1)S(1)} %copy-done.3), kind=kLoop, calls=%fused_computation.5 | loop fusion | flops 20970496 | bytes 17309696 | tf_op jit(solution)/shard_map/cond/branch_1_fun/reduce_sum | solution.py:92
  224.2 0.1 reduce_sum.18
  224.3 0.2 divide_convert_fusion
  224.5 2.2 convolution_convert_fusion.1
  226.7 0.9 copy.36
  227.5 0.7 copy.47
  (14 shorter events, 0.1 us)
Async XLA Ops:
  7.2 61.0 %copy-start = (bf16[8,128,512]{2,1,0:T(8,128)(2,1)S(1)}, bf16[8,128,512]{2,1,0:T(8,128)(2,1)}, u32[]{:S(2)}) copy-start(bf16[8,128,512]{2,1,0:T(8,128)(2,1)} %param.12) | copy-start | bytes 3145732
  7.2 180.7 %copy-start.1 = (s32[4096]{0:T(1024)S(1)}, s32[4096]{0:T(1024)}, u32[]{:S(2)}) copy-start(s32[4096]{0:T(1024)} %param.10) | copy-start | bytes 49156
  7.2 180.7 %all-gather.2.cloned.1.call-start = ((), (), s32[]{:S(2)}) async-start(), calls=%async_computation.1 | async-start | bytes 5406720 | tf_op jit(solution)/shard_map/all_gather | solution.py:73
  13.4 81.3 %all-to-all-start = ((bf16[32,4,576]{2,1,0:T(4,128)(2,1)}), bf16[32,4,576]{2,1,0:T(4,128)(2,1)S(1)}, u32[]{:S(2)}, u32[]{:S(2)}) async-start(bf16[32,4,576]{2,1,0:T(4,128)(2,1)} %reshape.219), calls=%async_computation | async-start | bytes 327680 | tf_op jit(solution)/shard_map/all_to_all | solution.py:44
  188.4 16.3 %copy-start.2 = (pred[128,4096]{1,0:T(8,128)(4,1)}, pred[128,4096]{1,0:T(8,128)(4,1)S(1)}, u32[]{:S(2)}) copy-start(pred[128,4096]{1,0:T(8,128)(4,1)S(1)} %compare_and_fusion) | copy-start | bytes 1572868 | tf_op jit(solution)/shard_map/cond
  204.7 10.4 %copy-start.3 = (pred[128,4096]{1,0:T(8,128)(4,1)S(1)}, pred[128,4096]{1,0:T(8,128)(4,1)}, u32[]{:S(2)}) copy-start(pred[128,4096]{1,0:T(8,128)(4,1)} %copy-done.2) | copy-start | bytes 1572868 | tf_op jit(solution)/shard_map/cond
Sparse Core Ops, SparseCore 0:
  10.7 177.1 all-gather.1
where the time goes:
time: 236 us; the launch traced here: 235 us
  waiting for transfers between devices  118 us (50%)
  starting transfers between devices  45.8 us (19%)
  matrix products  28.1 us (12%)
  between operations  17.3 us (7%)
  other arithmetic  14.7 us (6%)
  local copies, waits for them, and re-layouts  10.9 us (5%)
    all_gather x1, waiting for transfers between devices, on_device(): key_piece = lax.all_gather(latent_rows, 'ctx', axis=0, tiled=True)  93.2 us
    all_to_all x1, starting transfers between devices, ship_rows(): lax.all_to_all(outgoing, 'ctx', split_axis=0, concat_axis=0, tiled=True)  45.8 us
    all_to_all x1, waiting for transfers between devices, ship_rows(): lax.all_to_all(outgoing, 'ctx', split_axis=0, concat_axis=0, tiled=True)  24.9 us
    dot_general x1, matrix products, update(): jnp.einsum('qw,kw->qk', full_query, key_piece, preferred_element_type=jnp...  13.9 us
    dot_general x1, matrix products, update(): jnp.dot(weights.astype(jnp.bfloat16).reshape(row_count * local_heads, cou...  10.4 us
    reduce_sum x1, other arithmetic, update(): new_sum = jnp.sum(weights, axis=2)  9.08 us
  transfers between devices with their start and end apart: 2, of which 2 were waited for; matrix products, arithmetic and copies ran while one was open for 5% of the time, Pallas kernels for 0%

commit v1 on v0

--- a/solution.py
+++ b/solution.py
@@ -7,6 +7,12 @@
 ROPE = 64
 LATENT = 512
 VDIM = 128
+
+
+def gather_from_all(x, axis, dim):
+    size = lax.axis_size(axis)
+    repeats = [size if d == dim else 1 for d in range(x.ndim)]
+    return lax.all_to_all(jnp.tile(x, repeats), axis, split_axis=dim, concat_axis=dim, tiled=True)
 
 
 def rotate_pairs(rope_part, positions):
@@ -70,7 +76,7 @@
         jnp.zeros((row_count, local_heads), jnp.float32),
         jnp.zeros((row_count, local_heads, LATENT), jnp.float32),
     )
-    key_piece = lax.all_gather(latent_rows, "ctx", axis=0, tiled=True)
+    key_piece = gather_from_all(latent_rows, "ctx", 0)
     count = key_piece.shape[0]
     key_pos = jnp.arange(count, dtype=jnp.int32)
     is_live = (

time: 236 us -> 558 us (2.36)
  the two profiles are of different devices: /device:TPU:44 before, /device:TPU:96 now
where the time goes in v1:
time: 558 us; the launch traced here: 557 us
  waiting for transfers between devices  411 us (74%)
  blocking collectives  76.8 us (14%)
  matrix products  26.7 us (5%)
  local copies, waits for them, and re-layouts  17.7 us (3%)
  other arithmetic  14.7 us (3%)
  starting transfers between devices  6.5 us (1%)
    all_to_all x1, waiting for transfers between devices, gather_from_all(): lax.all_to_all(jnp.tile(x, repeats), axis, split_axis=dim, concat_axis=di...  411 us
    all_to_all x1, blocking collectives, ship_rows(): lax.all_to_all(outgoing, 'ctx', split_axis=0, concat_axis=0, tiled=True)  76.8 us
    dot_general x1, matrix products, update(): jnp.einsum('qw,kw->qk', full_query, key_piece, preferred_element_type=jnp...  14.3 us
  transfers between devices with their start and end apart: 1, of which 1 were waited for; matrix products, arithmetic and copies ran while one was open for 1% of the time, Pallas kernels for 0%

profile of v1, /device:TPU:96, one launch (start us, length us, event | category | flops | bytes accessed | tf_op | source)
XLA Modules:
  0.0 557.0 jit_solution(120054820477960833)
XLA Ops:
  0.6 0.0 copy-start
  0.6 0.8 fusion.20
  1.4 0.9 convert_reduce_fusion
  2.3 0.7 multiply_add_fusion
  3.0 1.1 convolution_convert_fusion.2
  4.1 0.2 copy.44
  4.3 0.1 reshape.227
  4.3 76.8 %all_to_all.13 = bf16[32,4,576]{2,1,0:T(4,128)(2,1)S(1)} all-to-all(bf16[32,4,576]{2,1,0:T(4,128)(2,1)S(1)} %reshape.227), channel_id=1, replica_groups=mesh['group'=2,'ctx'=32,'head'=4,'dec'=2] {'ctx'}, dimensions={0} | all-to-all | bytes 294912 | tf_op jit(solution)/shard_map/all_to_all | solution.py:50
  81.1 4.1 tile.2
  85.2 6.5 %all-to-all-start = ((bf16[32,128,576]{1,2,0:T(8,128)(2,1)}), bf16[32,128,576]{1,2,0:T(8,128)(2,1)}, u32[]{:S(2)}, u32[]{:S(2)}) async-start(bf16[32,128,576]{1,2,0:T(8,128)(2,1)} %tile.2), calls=%async_computation | async-start | bytes 9437184 | tf_op jit(solution)/shard_map/all_to_all | solution.py:15
  91.7 0.2 copy.37
  92.0 1.1 gather_fusion
  93.2 0.6 fusion.25
  93.7 0.7 fusion.24
  95.7 0.6 fusion.22
  98.2 0.1 multiply_cosine_fusion
  98.5 0.5 fusion.12
  99.0 1.1 pad_maximum_fusion
  100.1 410.7 %all-to-all-done = bf16[32,128,576]{1,2,0:T(8,128)(2,1)} async-done(((bf16[32,128,576]{1,2,0:T(8,128)(2,1)}), bf16[32,128,576]{1,2,0:T(8,128)(2,1)}, u32[]{:S(2)}, u32[]{:S(2)}) %all-to-all-start) | async-done | bytes 4718624 | tf_op jit(solution)/shard_map/all_to_all | solution.py:15
  510.7 42.4 %conditional.1 = (f32[128,8]{1,0:T(8,128)S(1)}, f32[128,8,512]{2,1,0:T(8,128)S(1)}) conditional(s32[]{:T(128)} %convert_element_type.40, () %tuple.16, (s32[4096]{0:T(1024)S(1)}, s32[128]{0:T(128)S(1)}, s32[4096]{0:T(1024)S(1)}, s32[128]{0:T(128)S(1)}, bf16[128,8,576]{0,2,1:T(8,128)(2,1)}, /*index=5*/bf16[32,128,576]{1,2,0:T(8,128)(2,1)}) %tuple.39), branch_computations={%region_3.4_spmd, %region_4.0_spmd} | conditional | flops 9182903296 | bytes 104268928 | solution.py:107
  510.7 0.5 compare_and_fusion
  511.2 0.0 copy-start.4
  511.2 7.9 %copy.41 = bf16[32,128,576]{2,1,0:T(8,128)(2,1)} copy(bf16[32,128,576]{1,2,0:T(8,128)(2,1)} %get-tuple-element.55) | data formatting | bytes 9437184 | tf_op jit(solution)/shard_map
  519.1 1.9 copy.40
  521.0 14.3 %fusion = (f32[1024]{0:T(1024)S(1)}, f32[1024,4096]{1,0:T(8,128)}) fusion(pred[128,4096]{1,0:T(8,128)(4,1)S(1)} %compare_and_fusion, bf16[4096,576]{1,0:T(8,128)(2,1)} %bitcast.48, bf16[128,8,576]{2,1,0:T(8,128)(2,1)} %copy.40), kind=kOutput, calls=%fused_computation.3 | convolution fusion | flops 4844420096 | bytes 23203840 | tf_op jit(solution)/shard_map/cond/branch_1_fun/qw,kw->qk/dot_general | solution.py:90
  535.3 8.6 %fusion.4 = f32[128,8,512]{2,1,0:T(8,128)S(1)} fusion(f32[1024,4096]{1,0:T(8,128)} %get-tuple-element.62, f32[1024]{0:T(1024)S(1)} %broadcast_maximum_fusion, pred[128,4096]{1,0:T(8,128)(4,1)} %copy-done.4, bf16[4096,576]{1,0:T(8,128)(2,1)S(1)} %bitcast.49), kind=kOutput, calls=%fused_computation.7 | convolution fusion | flops 4315938816 | bytes 23597056 | tf_op jit(solution)/shard_map/cond/branch_1_fun/dot_general | solution.py:99
  543.9 9.1 %fusion.2 = f32[1024]{0:T(1024)S(1)} fusion(f32[1024,4096]{1,0:T(8,128)} %get-tuple-element.62, f32[1024]{0:T(1024)S(1)} %broadcast_maximum_fusion, pred[128,4096]{1,0:T(8,128)(4,1)S(1)} %copy-done.5), kind=kLoop, calls=%fused_computation.5 | loop fusion | flops 20970496 | bytes 17309696 | tf_op jit(solution)/shard_map/cond/branch_1_fun/reduce_sum | solution.py:98
  553.0 0.1 reduce_sum.18
  553.1 0.2 divide_convert_fusion
  553.3 2.2 convolution_convert_fusion.1
  555.5 0.9 copy.45
  556.4 0.7 copy.56
  (19 shorter events, 0.1 us)
Async XLA Ops:
  0.6 97.8 %copy-start = (bf16[8,128,512]{2,1,0:T(8,128)(2,1)S(1)}, bf16[8,128,512]{2,1,0:T(8,128)(2,1)}, u32[]{:S(2)}) copy-start(bf16[8,128,512]{2,1,0:T(8,128)(2,1)} %param.12) | copy-start | bytes 3145732
  85.2 6.5 %copy-start.6 = (bf16[128,1536]{1,0:T(8,128)(2,1)S(1)}, bf16[128,1536]{1,0:T(8,128)(2,1)}, u32[]{:S(2)}) copy-start(bf16[128,1536]{1,0:T(8,128)(2,1)} %param.8) | copy-start | bytes 1179652
  85.2 6.8 %copy-start.1 = (s32[4096]{0:T(1024)S(1)}, s32[4096]{0:T(1024)}, u32[]{:S(2)}) copy-start(s32[4096]{0:T(1024)} %param.10) | copy-start | bytes 49156
  85.2 425.5 %all-to-all-start = ((bf16[32,128,576]{1,2,0:T(8,128)(2,1)}), bf16[32,128,576]{1,2,0:T(8,128)(2,1)}, u32[]{:S(2)}, u32[]{:S(2)}) async-start(bf16[32,128,576]{1,2,0:T(8,128)(2,1)} %tile.2), calls=%async_computation | async-start | bytes 9437184 | tf_op jit(solution)/shard_map/all_to_all | solution.py:15
  510.7 8.4 %copy-start.3 = (bf16[128,8,576]{0,2,1:T(8,128)(2,1)S(1)}, bf16[128,8,576]{0,2,1:T(8,128)(2,1)}, u32[]{:S(2)}) copy-start(bf16[128,8,576]{0,2,1:T(8,128)(2,1)} %get-tuple-element.54) | copy-start | bytes 3538948 | tf_op jit(solution)/shard_map/cond
  511.2 9.8 %copy-start.4 = (pred[128,4096]{1,0:T(8,128)(4,1)}, pred[128,4096]{1,0:T(8,128)(4,1)S(1)}, u32[]{:S(2)}) copy-start(pred[128,4096]{1,0:T(8,128)(4,1)S(1)} %compare_and_fusion) | copy-start | bytes 1572868 | tf_op jit(solution)/shard_map/cond
  521.0 14.3 %copy-start.2 = (bf16[32,128,576]{2,1,0:T(8,128)(2,1)S(1)}, bf16[32,128,576]{2,1,0:T(8,128)(2,1)}, u32[]{:S(2)}) copy-start(bf16[32,128,576]{2,1,0:T(8,128)(2,1)} %copy.41) | copy-start | bytes 14155780 | tf_op jit(solution)/shard_map/cond
  535.3 8.6 %copy-start.5 = (pred[128,4096]{1,0:T(8,128)(4,1)S(1)}, pred[128,4096]{1,0:T(8,128)(4,1)}, u32[]{:S(2)}) copy-start(pred[128,4096]{1,0:T(8,128)(4,1)} %copy-done.4) | copy-start | bytes 1572868 | tf_op jit(solution)/shard_map/cond
